TPU v7x, 32 devices: a whole 2x2x4 slice. The times are simulated.
32 devices in a mesh: grp: 4 (over y, x), zero: 8 (over z, core).
Axes of the slice: x: 2, y: 2, z: 4, core: 2. Of those that a mesh axis runs over, the one named last changes fastest.
Arguments:
- replica_grads: bfloat16 [4, 3072, 2, 12288], P('grp', None, None, 'zero'), may hold values from -20000 to 20000, as said below
- master_weights: float32 [3072, 2, 12288], P(('grp', 'zero')), may hold values from -0.6 to 0.6
- first_moment: float32 [3072, 2, 12288], P(('grp', 'zero')), may hold values from -0.3 to 0.3
- second_moment: float32 [3072, 2, 12288], P(('grp', 'zero')), may hold values from 0.001 to 0.03
- max_norm: float32 [1], replicated, may hold values from 1737.7856 to 4344.464
Outputs:
- new_master: float32 [3072, 2, 12288], P(('grp', 'zero'))
- new_first: float32 [3072, 2, 12288], P(('grp', 'zero'))
- new_second: float32 [3072, 2, 12288], P(('grp', 'zero'))
- new_weights: bfloat16 [3072, 2, 12288], P(None, None, 'zero')
Inputs may be any that keep to these rules, and one draw needn't show every extreme that they name: `replica_grads`: one gradient of the joined weight for each replica group.
All inputs are finite; a program needn't handle non-finite values.
Results may differ from a plain program's by a relative error of at most 0.015.
Values may be sent and summed in bfloat16 or wider, within the bound.
A program may use at most 192 MiB of HBM per device.

v0:
```python
import jax
import jax.numpy as jnp
from jax import lax
from jax.sharding import PartitionSpec as P

ADAM_STEP = 10
beta_one = 0.9
beta_two = 0.95
learn_rate = 0.02
adam_eps = 1e-08
norm_eps = 1e-06


def adam_update(summed, master, first, second, scale):
    clipped = summed * scale
    new_first = beta_one * first + (1.0 - beta_one) * clipped
    new_second = beta_two * second + (1.0 - beta_two) * clipped * clipped
    correct_one = 1.0 - beta_one**ADAM_STEP
    correct_two = 1.0 - beta_two**ADAM_STEP
    step_size = new_first / correct_one / (jnp.sqrt(new_second / correct_two) + adam_eps)
    new_master = master - learn_rate * step_size
    return (new_master, new_first, new_second)


def body(replica_grads, master_weights, first_moment, second_moment, max_norm):
    groups = lax.axis_size("grp")
    shards = lax.axis_size("zero")
    local_grad = replica_grads[0]
    local_width = local_grad.shape[2]
    rows_dev = master_weights.shape[0]
    full_width = master_weights.shape[2]
    blocks = local_grad.reshape(groups, shards, rows_dev, 2, local_width)
    arrived = lax.all_to_all(
        lax.all_to_all(blocks[None], "grp", split_axis=1, concat_axis=0, tiled=True),
        "zero",
        split_axis=2,
        concat_axis=5,
        tiled=True,
    )
    summed = jnp.sum(arrived.astype(jnp.float32), axis=0)
    summed = summed.reshape(master_weights.shape)
    total = lax.psum(jnp.sum(summed * summed), ("grp", "zero"))
    scale = jnp.minimum(jnp.float32(1.0), max_norm[0] / (jnp.sqrt(total) + norm_eps))
    new_master, new_first, new_second = adam_update(
        summed, master_weights, first_moment, second_moment, scale
    )
    fresh = new_master.astype(jnp.bfloat16).reshape(1, 1, rows_dev, 2, full_width)
    own_tiles = lax.all_to_all(fresh, "zero", split_axis=4, concat_axis=1, tiled=True)
    tiled = lax.all_gather(own_tiles, "grp", axis=0, tiled=True)
    new_weights = tiled.reshape(groups * shards * rows_dev, 2, full_width // shards)
    return (new_master, new_first, new_second, new_weights)


def solution(mesh):
    in_specs = (
        P("grp", None, None, "zero"),
        P(("grp", "zero"), None, None),
        P(("grp", "zero"), None, None),
        P(("grp", "zero"), None, None),
        P(),
    )
    out_specs = (
        P(("grp", "zero"), None, None),
        P(("grp", "zero"), None, None),
        P(("grp", "zero"), None, None),
        P(None, None, "zero"),
    )
    return jax.shard_map(body, mesh=mesh, in_specs=in_specs, out_specs=out_specs, check_vma=False)
```

profile of v0, /device:TPU:0, one launch (start us, length us, event | category | flops | bytes accessed | tf_op | source)
XLA Modules:
  0.0 1264.3 jit_solution(17715620397299692491)
XLA Ops:
  7.2 0.0 all-gather.3.cloned.1.call-start
  7.2 218.8 %all_to_all.39 = bf16[1,4,8,96,2,1536]{5,4,3,2,0,1:T(2,128)(2,1)} all-to-all(bf16[1,4,8,96,2,1536]{5,4,3,2,0,1:T(2,128)(2,1)} %bitcast.20), channel_id=1, replica_groups=mesh['grp'=4,'zero'=8] {'grp'}, dimensions={1} | all-to-all | bytes 37748736 | tf_op jit(solution)/shard_map/all_to_all | solution.py:34
  226.0 15.4 %copy.48 = bf16[4,1,8,96,2,1536]{5,4,3,0,1,2:T(2,128)(2,1)S(1)} copy(bf16[4,1,8,96,2,1536]{5,4,3,2,0,1:T(2,128)(2,1)} %bitcast.16) | data formatting | bytes 37748736 | tf_op jit(solution)/shard_map/all_to_all | solution.py:34
  241.4 413.5 %all_to_all.40 = bf16[4,1,8,96,2,1536]{5,4,3,0,1,2:T(2,128)(2,1)} all-to-all(bf16[4,1,8,96,2,1536]{5,4,3,0,1,2:T(2,128)(2,1)S(1)} %copy.48), channel_id=1, replica_groups=mesh['grp'=4,'zero'=8] {'zero'}, dimensions={2} | all-to-all | bytes 37748736 | tf_op jit(solution)/shard_map/all_to_all | solution.py:33
  654.9 17.5 %convert_reduce_fusion = f32[8,96,2,1536]{3,1,2,0:T(8,128)} fusion(bf16[4,1,8,96,2,1536]{5,4,3,0,1,2:T(2,128)(2,1)} %all_to_all.40), kind=kLoop, calls=%fused_computation | loop fusion | flops 16515072 | bytes 28311552 | tf_op jit(solution)/shard_map/reduce_sum | solution.py:40
  672.5 14.0 %multiply_reduce_fusion = f32[]{:T(128)} fusion(f32[8,96,2,1536]{3,1,2,0:T(8,128)} %convert_reduce_fusion), kind=kLoop, calls=%fused_computation.8 | loop fusion | flops 4718591 | bytes 9437188 | tf_op jit(solution)/shard_map/reduce_sum | solution.py:42
  687.1 38.2 %psum.7 = f32[]{:T(128)} all-reduce(f32[]{:T(128)} %multiply_reduce_fusion), channel_id=1, replica_groups=mesh['grp'=4,'zero'=8] {'grp','zero'}, use_global_device_ids=true, to_apply=%region_2.0 | all-reduce | flops 1 | bytes 8 | tf_op jit(solution)/shard_map/psum | solution.py:42
  726.0 16.1 %multiply_bitcast_fusion = f32[96,2,8,1536]{3,1,0,2:T(2,128)S(1)} fusion(f32[8,96,2,1536]{3,1,2,0:T(8,128)} %convert_reduce_fusion, f32[]{:T(128)S(6)} %min_shard_map.3), kind=kLoop, calls=%fused_computation.7 | loop fusion | flops 2359296 | bytes 18874372 | tf_op jit(solution)/shard_map/mul | solution.py:15
  742.1 9.2 copy.51
  751.3 10.0 mul.56
  761.3 33.4 %convert_bitcast_fusion = (bf16[1,1,96,2,12288]{4,2,3,1,0:T(8,128)(2,1)}, f32[96,2,12288]{2,0,1:T(8,128)}, f32[96,2,12288]{2,0,1:T(8,128)}, f32[96,2,12288]{2,0,1:T(8,128)}) fusion(f32[96,2,12288]{2,1,0:T(2,128)} %param.6, f32[96,2,12288]{2,0,1:T(8,128)} %mul.56, f32[96,2,12288]{2,1,0:T(2,128)} %param.7, f32[96,2,12288]{2,1,0:T(2,128)} %param.8), kind=kLoop, calls=%fused_computation.9 | loop fusion | flops 33030144 | bytes 70778880 | tf_op jit(solution)/shard_map/reshape | solution.py:47
  794.7 14.1 %copy.54 = bf16[1,1,96,2,12288]{2,3,1,0,4:T(2,128)(2,1)} copy(bf16[1,1,96,2,12288]{4,2,3,1,0:T(8,128)(2,1)} %get-tuple-element.20) | data formatting | bytes 9437184 | tf_op jit(solution)/shard_map/reshape | solution.py:47
  808.8 144.7 %all_to_all.41 = bf16[1,1,96,2,12288]{2,3,1,0,4:T(2,128)(2,1)} all-to-all(bf16[1,1,96,2,12288]{2,3,1,0,4:T(2,128)(2,1)} %copy.54), channel_id=1, replica_groups=mesh['grp'=4,'zero'=8] {'zero'}, dimensions={4} | all-to-all | bytes 9437184 | tf_op jit(solution)/shard_map/all_to_all | solution.py:48
  953.5 15.8 %copy.55 = bf16[1,1,96,2,8,1536]{5,2,3,1,4,0:T(8,128)(2,1)} copy(bf16[1,1,96,2,8,1536]{2,3,5,4,1,0:T(2,128)(2,1)} %bitcast.19) | data formatting | bytes 9437184 | tf_op jit(solution)/shard_map/all_to_all | solution.py:48
  969.3 0.0 all-gather.3.cloned.1.call-update
  969.3 0.0 slice-start
  969.3 0.0 slice-start.1
  969.3 17.2 %copy.57 = f32[96,2,12288]{2,1,0:T(2,128)} copy(f32[96,2,12288]{2,0,1:T(8,128)} %get-tuple-element.21) | data formatting | bytes 18874368
  986.6 0.0 slice-start.2
  986.6 17.1 %copy.58 = f32[96,2,12288]{2,1,0:T(2,128)} copy(f32[96,2,12288]{2,0,1:T(8,128)} %get-tuple-element.22) | data formatting | bytes 18874368
  1003.7 0.0 slice-done
  1003.7 0.0 slice-done.1
  1003.7 0.0 slice-done.2
  1003.7 16.1 %copy.59 = f32[96,2,12288]{2,1,0:T(2,128)} copy(f32[96,2,12288]{2,0,1:T(8,128)S(1)} %bitcast.18) | data formatting | bytes 18874368
  1019.8 124.6 %all-gather.3.cloned.1.call-done = bf16[4,8,1,96,2,1536]{5,3,4,2,1,0:T(8,128)(2,1)} async-done(((bf16[1,8,1,96,2,1536]{5,3,4,2,1,0:T(8,128)(2,1)}), bf16[4,8,1,96,2,1536]{5,3,4,2,1,0:T(8,128)(2,1)}) %all-gather.3.cloned.1.call-update) | async-done | bytes 18874384 | tf_op jit(solution)/shard_map/all_gather | solution.py:49
  1144.4 9.5 copy.56
  1153.9 103.4 %copy.60 = bf16[3072,2,1536]{2,1,0:T(2,128)(2,1)} copy(bf16[3072,2,1536]{2,0,1:T(8,128)(2,1)S(1)} %bitcast.15) | data formatting | bytes 37748736
  (1 shorter events, 0.0 us)
Async XLA Ops:
  7.2 1137.2 %all-gather.3.cloned.1.call-start = ((), (), s32[]{:S(2)}) async-start(), calls=%async_computation.3 | async-start | bytes 23592960 | tf_op jit(solution)/shard_map/all_gather | solution.py:49
  969.3 34.4 %slice-start = ((s8[9437184]{0:T(1024)(128)(4,1)}), s8[4194304]{0:T(1024)(128)(4,1)S(1)}, s32[]{:S(2)}) async-start(s8[9437184]{0:T(1024)(128)(4,1)} %bitcast.17), calls=%async_computation.4 | async-start | bytes 8388608
  969.3 34.4 %slice-start.1 = ((s8[9437184]{0:T(1024)(128)(4,1)}), s8[4194304]{0:T(1024)(128)(4,1)S(1)}, s32[]{:S(2)}) async-start(s8[9437184]{0:T(1024)(128)(4,1)} %bitcast.17), calls=%async_computation.5 | async-start | bytes 8388608
  986.6 17.2 %slice-start.2 = ((s8[9437184]{0:T(1024)(128)(4,1)}), s8[1048576]{0:T(1024)(128)(4,1)S(1)}, s32[]{:S(2)}) async-start(s8[9437184]{0:T(1024)(128)(4,1)} %bitcast.17), calls=%async_computation.6 | async-start | bytes 2097152
Sparse Core Ops, SparseCore 0:
  969.4 174.8 all-gather.2
where the time goes:
time: 1270 us; the launch traced here: 1260 us
  blocking collectives  815 us (64%)
  local copies, waits for them, and re-layouts  228 us (18%)
  waiting for transfers between devices  125 us (10%)
  other arithmetic  81 us (6%)
  between operations  15.7 us (1%)
    all_to_all x1, blocking collectives, body(): lax.all_to_all(lax.all_to_all(blocks[None], 'grp', split_axis=1, concat_a...  414 us
    all_to_all x1, blocking collectives, body(): lax.all_to_all(blocks[None], 'grp', split_axis=1, concat_axis=0, tiled=True)  219 us
    unnamed x10, local copies, waits for them, and re-layouts  154 us
    all_to_all x1, blocking collectives, body(): lax.all_to_all(fresh, 'zero', split_axis=4, concat_axis=1, tiled=True)  145 us
    all_gather x1, waiting for transfers between devices, body(): tiled = lax.all_gather(own_tiles, 'grp', axis=0, tiled=True)  125 us
    psum x1, blocking collectives, body(): total = lax.psum(jnp.sum(summed * summed), ('grp', 'zero'))  38.2 us
    reshape x1, other arithmetic, body(): new_master.astype(jnp.bfloat16).reshape(1, 1, rows_dev, 2, full_width)  33.4 us
  transfers between devices with their start and end apart: 1, of which 1 were waited for; matrix products, arithmetic and copies ran while one was open for 4% of the time, Pallas kernels for 0%

commit v1 on v0

--- a/solution.py
+++ b/solution.py
@@ -45,7 +45,10 @@
         summed, master_weights, first_moment, second_moment, scale
     )
     fresh = new_master.astype(jnp.bfloat16).reshape(1, 1, rows_dev, 2, full_width)
-    own_tiles = lax.all_to_all(fresh, "zero", split_axis=4, concat_axis=1, tiled=True)
+    own_tiles = jnp.concatenate(
+        lax.all_to_all(jnp.stack(jnp.split(fresh, lax.axis_size("zero"), axis=4)), "zero", 0, 0),
+        axis=1,
+    )
     tiled = lax.all_gather(own_tiles, "grp", axis=0, tiled=True)
     new_weights = tiled.reshape(groups * shards * rows_dev, 2, full_width // shards)
     return (new_master, new_first, new_second, new_weights)

time: 1270 us -> 1200 us (0.945)
  blocking collectives: 815 us -> 780 us
  local copies, waits for them, and re-layouts: 228 us -> 198 us
    all_to_all x1, blocking collectives: 145 us -> 109 us  [body(): lax.all_to_all(jnp.stack(jnp.split(fresh, lax.axis_size('zero'), axis=4))...]
    all_to_all x1 -> x0, local copies, waits for them, and re-layouts: 15.8 us -> none  [body(): lax.all_to_all(fresh, 'zero', split_axis=4, concat_axis=1, tiled=True)]
    reshape x1 -> x0, local copies, waits for them, and re-layouts: 14.1 us -> none  [body(): new_master.astype(jnp.bfloat16).reshape(1, 1, rows_dev, 2, full_width)]
    unnamed x10 -> x17, local copies, waits for them, and re-layouts: 154 us -> 154 us
where the time goes in v1:
time: 1200 us
  blocking collectives  780 us (65%)
  local copies, waits for them, and re-layouts  198 us (16%)
  waiting for transfers between devices  125 us (10%)
  other arithmetic  79.7 us (7%)
  between operations  15.8 us (1%)
    all_to_all x1, blocking collectives, body(): lax.all_to_all(lax.all_to_all(blocks[None], 'grp', split_axis=1, concat_a...  414 us
    all_to_all x1, blocking collectives, body(): lax.all_to_all(blocks[None], 'grp', split_axis=1, concat_axis=0, tiled=True)  219 us
    unnamed x17, local copies, waits for them, and re-layouts  154 us
    all_gather x1, waiting for transfers between devices, body(): tiled = lax.all_gather(own_tiles, 'grp', axis=0, tiled=True)  125 us
    all_to_all x1, blocking collectives, body(): lax.all_to_all(jnp.stack(jnp.split(fresh, lax.axis_size('zero'), axis=4))...  109 us
    psum x1, blocking collectives, body(): total = lax.psum(jnp.sum(summed * summed), ('grp', 'zero'))  38.2 us
    reshape x1, other arithmetic, body(): new_master.astype(jnp.bfloat16).reshape(1, 1, rows_dev, 2, full_width)  32.1 us
  transfers between devices with their start and end apart: 1, of which 1 were waited for; matrix products, arithmetic and copies ran while one was open for 4% of the time, Pallas kernels for 0%

profile of v1, /device:TPU:0, one launch (start us, length us, event | category | flops | bytes accessed | tf_op | source)
XLA Modules:
  0.0 1198.1 jit_solution(150609943634955342)
XLA Ops:
  7.2 0.0 all-gather.3.cloned.1.call-start
  7.2 218.8 %all_to_all.26 = bf16[1,4,8,96,2,1536]{5,4,3,2,0,1:T(2,128)(2,1)} all-to-all(bf16[1,4,8,96,2,1536]{5,4,3,2,0,1:T(2,128)(2,1)} %bitcast.49), channel_id=1, replica_groups=mesh['grp'=4,'zero'=8] {'grp'}, dimensions={1} | all-to-all | bytes 37748736 | tf_op jit(solution)/shard_map/all_to_all | solution.py:34
  226.0 15.4 %copy.29 = bf16[4,1,8,96,2,1536]{5,4,3,0,1,2:T(2,128)(2,1)S(1)} copy(bf16[4,1,8,96,2,1536]{5,4,3,2,0,1:T(2,128)(2,1)} %bitcast.46) | data formatting | bytes 37748736 | tf_op jit(solution)/shard_map/all_to_all | solution.py:34
  241.4 413.5 %all_to_all.27 = bf16[4,1,8,96,2,1536]{5,4,3,0,1,2:T(2,128)(2,1)} all-to-all(bf16[4,1,8,96,2,1536]{5,4,3,0,1,2:T(2,128)(2,1)S(1)} %copy.29), channel_id=1, replica_groups=mesh['grp'=4,'zero'=8] {'zero'}, dimensions={2} | all-to-all | bytes 37748736 | tf_op jit(solution)/shard_map/all_to_all | solution.py:33
  654.9 17.5 %convert_reduce_fusion = f32[8,96,2,1536]{3,1,2,0:T(8,128)} fusion(bf16[4,1,8,96,2,1536]{5,4,3,0,1,2:T(2,128)(2,1)} %all_to_all.27), kind=kLoop, calls=%fused_computation | loop fusion | flops 16515072 | bytes 28311552 | tf_op jit(solution)/shard_map/reduce_sum | solution.py:40
  672.5 14.0 %multiply_reduce_fusion = f32[]{:T(128)} fusion(f32[8,96,2,1536]{3,1,2,0:T(8,128)} %convert_reduce_fusion), kind=kLoop, calls=%fused_computation.8 | loop fusion | flops 4718591 | bytes 9437188 | tf_op jit(solution)/shard_map/reduce_sum | solution.py:42
  687.1 38.2 %psum.7 = f32[]{:T(128)} all-reduce(f32[]{:T(128)} %multiply_reduce_fusion), channel_id=1, replica_groups=mesh['grp'=4,'zero'=8] {'grp','zero'}, use_global_device_ids=true, to_apply=%region_2.0 | all-reduce | flops 1 | bytes 8 | tf_op jit(solution)/shard_map/psum | solution.py:42
  726.0 16.1 %multiply_bitcast_fusion = f32[96,2,8,1536]{3,1,0,2:T(2,128)S(1)} fusion(f32[8,96,2,1536]{3,1,2,0:T(8,128)} %convert_reduce_fusion, f32[]{:T(128)S(6)} %min_shard_map.3), kind=kLoop, calls=%fused_computation.7 | loop fusion | flops 2359296 | bytes 18874372 | tf_op jit(solution)/shard_map/mul | solution.py:15
  742.1 9.2 copy.32
  751.3 10.0 mul.56
  761.3 32.1 %convert_bitcast_fusion = (bf16[1,1,96,2,12288]{4,2,3,1,0:T(8,128)(2,1)S(1)}, f32[96,2,12288]{2,0,1:T(8,128)}, f32[96,2,12288]{2,0,1:T(8,128)}, f32[96,2,12288]{2,0,1:T(8,128)}) fusion(f32[96,2,12288]{2,1,0:T(2,128)} %param.6, f32[96,2,12288]{2,0,1:T(8,128)} %mul.56, f32[96,2,12288]{2,1,0:T(2,128)} %param.7, f32[96,2,12288]{2,1,0:T(2,128)} %param.8), kind=kLoop, calls=%fused_computation.9 | loop fusion | flops 33030144 | bytes 70778880 | tf_op jit(solution)/shard_map/reshape | solution.py:47
  793.8 109.1 %all_to_all.28 = bf16[8,1,1,96,2,1536]{5,3,4,2,1,0:T(8,128)(2,1)} all-to-all(bf16[8,1,1,96,2,1536]{5,3,4,2,1,0:T(8,128)(2,1)S(1)} %fusion.2), channel_id=1, replica_groups=mesh['grp'=4,'zero'=8] {'zero'}, dimensions={0} | all-to-all | bytes 9437184 | tf_op jit(solution)/shard_map/all_to_all | solution.py:49
  902.9 0.0 all-gather.3.cloned.1.call-update
  903.0 0.0 slice-start
  903.0 0.0 slice-start.1
  903.0 17.2 %copy.36 = f32[96,2,12288]{2,1,0:T(2,128)} copy(f32[96,2,12288]{2,0,1:T(8,128)} %get-tuple-element.17) | data formatting | bytes 18874368
  920.2 0.0 slice-start.2
  920.2 17.1 %copy.37 = f32[96,2,12288]{2,1,0:T(2,128)} copy(f32[96,2,12288]{2,0,1:T(8,128)} %get-tuple-element.18) | data formatting | bytes 18874368
  937.3 0.0 slice-done
  937.3 0.0 slice-done.1
  937.3 0.0 slice-done.2
  937.4 16.1 %copy.38 = f32[96,2,12288]{2,1,0:T(2,128)} copy(f32[96,2,12288]{2,0,1:T(8,128)S(1)} %bitcast.48) | data formatting | bytes 18874368
  953.5 124.7 %all-gather.3.cloned.1.call-done = bf16[32,1,1,96,2,1536]{5,3,4,2,1,0:T(8,128)(2,1)} async-done(((bf16[8,1,1,96,2,1536]{5,3,4,2,1,0:T(8,128)(2,1)}), bf16[32,1,1,96,2,1536]{5,3,4,2,1,0:T(8,128)(2,1)}) %all-gather.3.cloned.1.call-update) | async-done | bytes 18874384 | tf_op jit(solution)/shard_map/all_gather | solution.py:52
  1078.1 9.5 copy.35
  1087.6 103.4 %copy.39 = bf16[3072,2,1536]{2,1,0:T(2,128)(2,1)} copy(bf16[3072,2,1536]{2,0,1:T(8,128)(2,1)S(1)} %bitcast.45) | data formatting | bytes 37748736
  (9 shorter events, 0.3 us)
Async XLA Ops:
  7.2 1071.0 %all-gather.3.cloned.1.call-start = ((), (), s32[]{:S(2)}) async-start(), calls=%async_computation.3 | async-start | bytes 23592960 | tf_op jit(solution)/shard_map/all_gather | solution.py:52
  903.0 34.4 %slice-start = ((s8[9437184]{0:T(1024)(128)(4,1)}), s8[4194304]{0:T(1024)(128)(4,1)S(1)}, s32[]{:S(2)}) async-start(s8[9437184]{0:T(1024)(128)(4,1)} %bitcast.47), calls=%async_computation.4 | async-start | bytes 8388608
  903.0 34.4 %slice-start.1 = ((s8[9437184]{0:T(1024)(128)(4,1)}), s8[4194304]{0:T(1024)(128)(4,1)S(1)}, s32[]{:S(2)}) async-start(s8[9437184]{0:T(1024)(128)(4,1)} %bitcast.47), calls=%async_computation.5 | async-start | bytes 8388608
  920.2 17.2 %slice-start.2 = ((s8[9437184]{0:T(1024)(128)(4,1)}), s8[1048576]{0:T(1024)(128)(4,1)S(1)}, s32[]{:S(2)}) async-start(s8[9437184]{0:T(1024)(128)(4,1)} %bitcast.47), calls=%async_computation.6 | async-start | bytes 2097152
Sparse Core Ops, SparseCore 0:
  903.1 174.9 all-gather.2
